TPU v7x, 32 devices: a whole 2x2x4 slice. The times are simulated.
32 devices in a mesh: seq: 8 (over z, y), head: 4 (over x, core).
Axes of the slice: x: 2, y: 2, z: 4, core: 2. Of those that a mesh axis runs over, the one named last changes fastest.
Arguments:
- cache: bfloat16 [1024, 576], P('seq'), may hold values from -8 to 8
- query_nope: bfloat16 [1024, 4096], P('seq', 'head'), may hold values from -5 to 5
- query_rope: bfloat16 [1024, 2048], P('seq', 'head'), may hold values from -256 to 256
- scale_exp: int32 [1024], P('seq'), may hold values from -1 to 1
- offsets: int32 [16], P('seq'), may hold values from 0 to 960
- up_key: bfloat16 [512, 4096], P(None, 'head'), may hold values from -0.25 to 0.25
- up_value: bfloat16 [512, 4096], P(None, 'head'), may hold values from -0.25 to 0.25
- grad_out: bfloat16 [1024, 4096], P('seq', 'head'), may hold values from -5 to 5
Outputs:
- d_cache: bfloat16 [1024, 576], P('seq')
- d_query_nope: bfloat16 [1024, 4096], P('seq', 'head')
- d_query_rope: bfloat16 [1024, 2048], P('seq', 'head')
All inputs are finite; a program needn't handle non-finite values.
Results may differ from a plain program's by a relative error of at most 0.0099.
Values may be sent and summed in bfloat16 or wider, within the bound.
A program may use at most 64 MiB of HBM per device.

v0:
```python
import functools
import math

import jax
import jax.numpy as jnp
from jax import lax
from jax.experimental import pallas as pl
from jax.experimental.pallas import tpu as pltpu
from jax.sharding import PartitionSpec as P

LATENT = 512
ROPE = 64
NOPE = 128
QBLOCK = 64
MESH = pl.DeviceIdType.MESH
BF16 = jnp.bfloat16
F32 = jnp.float32
NEG = -1e30


def dot(a, b):
    return jnp.dot(a, b, preferred_element_type=F32)


def dot_nt(a, b):
    return lax.dot_general(a, b, (((1,), (1,)), ((), ())), preferred_element_type=F32)


def kernel(
    nz, nx,
    cache_ref, qn_ref, qr_ref, se_ref, off_ref, uk_ref, uv_ref, go_ref,
    dc_ref, dqn_ref, dqr_ref,
    full, cT, extT, ext, backT, back, upkT, S, dP, pT, dsT, mx, D,
    csnd, crcv, ysnd, yrcv, zsnd, zrcv, xsnd, xrcv, fin, rfin,
    gz_send, gy_send, gc_send, g_recv,
    c_send, c_recv, y_send, y_recv, z_send, z_recv, x_send, x_recv, f_send, f_recv,
):
    own, width = cache_ref.shape
    half = own // 2
    pair = 2 * own
    queries = qn_ref.shape[0]
    heads = qn_ref.shape[1] // NOPE
    rows = heads * queries
    scale = (NOPE + ROPE) ** (-0.5)
    s_me = lax.axis_index("seq")
    h_me = lax.axis_index("head")
    z, y = s_me // 2, lax.rem(s_me, 2)
    x, core = h_me // 2, lax.rem(h_me, 2)
    oy, oc = 1 - y, 1 - core

    def z_dev(zz):
        return (zz * 2 + y, h_me)

    y_dev = (z * 2 + oy, h_me)
    c_dev = (s_me, x * 2 + oc)

    def x_dev(xx):
        return (s_me, xx * 2 + core)

    zs = [lax.rem(z + k, nz) for k in range(nz)]
    xs = [lax.rem(x + k, nx) for k in range(nx)]

    barrier = pltpu.get_barrier_semaphore()
    peers = [z_dev(zz) for zz in zs[1:]] + [y_dev, c_dev] + [x_dev(xx) for xx in xs[1:]]
    for dev in peers:
        pl.semaphore_signal(barrier, inc=1, device_id=dev, device_id_type=MESH)
    pl.semaphore_wait(barrier, len(peers))

    def remote(src, dst, send, recv, dev):
        return pltpu.make_async_remote_copy(
            src_ref=src, dst_ref=dst, send_sem=send, recv_sem=recv,
            device_id=dev, device_id_type=MESH,
        )

    def half_rows(blk, hf):
        return pl.ds(pl.multiple_of(blk * own + hf * half, half), half)

    def gather(src, blk, hf, send, dev):
        return remote(src, full.at[half_rows(blk, hf)], send, g_recv.at[blk * 2 + hf], dev)

    sends = []
    mine = cache_ref.at[pl.ds(pl.multiple_of(core * half, half), half)]

    def go(copy):
        copy.start()
        sends.append(copy)

    go(gather(mine, s_me, core, gy_send.at[0], y_dev))
    for k in range(1, nz):
        go(gather(mine, s_me, core, gz_send.at[k], z_dev(zs[k])))

    full[pl.ds(pl.multiple_of(s_me * own, own), own), :] = cache_ref[...]
    factor = jnp.exp2(se_ref[...].astype(F32))
    lane = lax.broadcasted_iota(jnp.int32, (1, queries), 1)
    pos = jnp.zeros((1, queries), jnp.int32)
    for b in range(queries // QBLOCK):
        inside = (lane >= b * QBLOCK) & (lane < (b + 1) * QBLOCK)
        pos = jnp.where(inside, off_ref[b] + lane - b * QBLOCK, pos)

    for h in range(heads):
        cols = slice(h * NOPE, (h + 1) * NOPE)
        qs = slice(h * queries, (h + 1) * queries)
        w = uk_ref[:, cols]
        a = (dot_nt(w, qn_ref[:, cols]) * factor).astype(BF16)
        extT[0:LATENT, qs] = a
        ext[qs, 0:LATENT] = a.T
        upkT[cols, :] = w.T
        g = dot_nt(uv_ref[:, cols], go_ref[:, cols]).astype(BF16)
        backT[:, qs] = g
        back[qs, :] = g.T
    for h in range(0, heads, 2):
        r = (qr_ref[:, h * ROPE : (h + 2) * ROPE].astype(F32).T * factor).astype(BF16)
        for i in range(2):
            part = r[i * ROPE : (i + 1) * ROPE, :]
            qs = slice((h + i) * queries, (h + i + 1) * queries)
            extT[LATENT:width, qs] = part
            ext[qs, LATENT:width] = part.astype(F32).T.astype(BF16)
    mx[...] = jnp.full(mx.shape, NEG, F32)

    tile = 2 * queries
    pos2 = jnp.concatenate([pos, pos], axis=1)

    def scores(zz):
        base = pl.multiple_of(zz * pair, pair)
        c = full[pl.ds(base, pair), :]
        key = base + lax.broadcasted_iota(jnp.int32, (pair, tile), 0)
        seen = key <= pos2
        for t in range(rows // tile):
            ls = slice(t * tile, (t + 1) * tile)
            s = dot(c, extT[:, ls]) * (scale * math.log2(math.e))
            s = jnp.where(seen, s, NEG)
            S[pl.ds(base, pair), ls] = s
            mx[:, ls] = jnp.maximum(mx[:, ls], jnp.max(s.reshape(pair // 8, 8, tile), axis=0))
            dP[pl.ds(base, pair), ls] = dot(c[:, :LATENT], backT[:, ls])
        cT[:, pl.ds(base, pair)] = c.T

    def got(blk, hf):
        gather(mine, blk, hf, gy_send.at[0], c_dev).wait_recv()

    def forward(blk, send, dev):
        go(gather(full.at[half_rows(blk, core)], blk, core, send, dev))

    for k in range(nz + 2):
        if 1 <= k < nz:
            blk = zs[k] * 2 + y
            got(blk, core)
            forward(blk, gy_send.at[k], y_dev)
            forward(blk, gc_send.at[k], c_dev)
        if 1 <= k <= nz:
            blk = zs[k - 1] * 2 + oy
            got(blk, core)
            forward(blk, gc_send.at[nz + k - 1], c_dev)
        if k >= 2:
            zz = zs[k - 2]
            if k > 2:
                got(zz * 2 + y, oc)
            got(zz * 2 + oy, oc)
            scores(zz)

    keys = full.shape[0]
    chunk = own

    def soften(h, carry):
        ls = pl.ds(pl.multiple_of(h * queries, queries), queries)
        top = jnp.max(mx[:, ls], axis=0, keepdims=True)
        tot = jnp.zeros((8, queries), F32)
        dl = jnp.zeros((8, queries), F32)
        for i in range(keys // chunk):
            rs = slice(i * chunk, (i + 1) * chunk)
            p = jnp.exp2(S[rs, ls] - top)
            S[rs, ls] = p
            tot = tot + jnp.sum(p.reshape(chunk // 8, 8, queries), axis=0)
            dl = dl + jnp.sum((p * dP[rs, ls]).reshape(chunk // 8, 8, queries), axis=0)
        inv = 1.0 / jnp.sum(tot, axis=0, keepdims=True)
        delta = jnp.sum(dl, axis=0, keepdims=True) * inv
        for i in range(keys // chunk):
            rs = slice(i * chunk, (i + 1) * chunk)
            pr = S[rs, ls] * inv
            pT[rs, ls] = pr.astype(BF16)
            dsT[rs, ls] = (pr * (dP[rs, ls] - delta) * scale).astype(BF16)
        return carry

    lax.fori_loop(0, heads, soften, 0)

    def core_copy(zz, i):
        return remote(csnd.at[zz], crcv.at[zz], c_send.at[zz], c_recv.at[zz], c_dev)

    def y_copy(zz):
        return remote(ysnd.at[zz], yrcv.at[zz], y_send.at[zz], y_recv.at[zz], y_dev)

    def step_d(k):
        zz = zs[k]
        rs = pl.ds(pl.multiple_of(zz * pair, pair), pair)
        ds, pb = dsT[rs, :], pT[rs, :]
        D[rs, 0:LATENT] = dot(ds, ext[:, 0:LATENT]) + dot(pb, back[...])
        D[rs, LATENT:width] = dot(ds, ext[:, LATENT:width])
        for yy in range(2):
            csnd[zz, yy] = D[half_rows(zz * 2 + yy, oc), :].astype(BF16)
        go(core_copy(zz, 0))

    def step_e(k):
        zz = zs[k]
        core_copy(zz, 0).wait_recv()
        t = D[half_rows(zz * 2 + oy, core), :] + crcv[zz, oy].astype(F32)
        ysnd[zz] = t.astype(BF16)
        go(y_copy(zz))

    def step_f(k):
        zz = zs[k]
        y_copy(zz).wait_recv()
        u = (
            D[half_rows(zz * 2 + y, core), :]
            + crcv[zz, y].astype(F32)
            + yrcv[zz].astype(F32)
        )
        if k:
            zsnd[zz] = u.astype(BF16)
            go(remote(zsnd.at[zz], zrcv.at[z], z_send.at[zz], z_recv.at[z], z_dev(zz)))
        return u

    def grads(h):
        g = dot(cT[...], dsT[:, h * queries : (h + 2) * queries])
        lo = g[0:LATENT].astype(BF16)
        hi = g[LATENT:width]
        ropes = []
        for i in range(2):
            qs = slice(i * queries, (i + 1) * queries)
            cols = slice((h + i) * NOPE, (h + i + 1) * NOPE)
            d = dot(upkT[cols, :], lo[:, qs]) * factor
            dqn_ref[:, cols] = d.T.astype(BF16)
            ropes.append(hi[:, qs] * factor)
        dqr_ref[:, h * ROPE : (h + 2) * ROPE] = jnp.concatenate(ropes, axis=0).T.astype(BF16)

    order = list(range(1, nz)) + [0]
    pieces = list(range(0, heads, 2))
    for i, k in enumerate(order):
        step_d(k)
        if i:
            step_e(order[i - 1])
    grads(pieces.pop(0))
    step_e(order[-1])
    for k in order[:-1]:
        step_f(k)
        if pieces:
            grads(pieces.pop(0))
    while pieces:
        grads(pieces.pop(0))
    v = step_f(0)
    for k in range(1, nz):
        remote(
            zsnd.at[zs[k]], zrcv.at[zs[k]], z_send.at[zs[k]], z_recv.at[zs[k]], z_dev(zs[k])
        ).wait_recv()
        v = v + zrcv[zs[k]].astype(F32)
    vb = v.astype(BF16)
    xsnd[...] = vb
    for k in range(1, nx):
        go(remote(xsnd, xrcv.at[x], x_send.at[xs[k]], x_recv.at[x], x_dev(xs[k])))
    xrcv[x] = vb
    for k in range(1, nx):
        remote(
            xsnd, xrcv.at[xs[k]], x_send.at[xs[k]], x_recv.at[xs[k]], x_dev(xs[k])
        ).wait_recv()
    w = xrcv[0].astype(F32)
    for i in range(1, nx):
        w = w + xrcv[i].astype(F32)
    wb = w.astype(BF16)
    fin[...] = wb
    last = remote(fin, rfin, f_send.at[0], f_recv.at[0], c_dev)
    go(last)
    dc_ref[pl.ds(pl.multiple_of(core * half, half), half), :] = wb
    last.wait_recv()
    dc_ref[pl.ds(pl.multiple_of(oc * half, half), half), :] = rfin[...]
    for copy in sends:
        copy.wait_send()


def solution(mesh):
    seq, head = mesh.shape["seq"], mesh.shape["head"]
    nz, nx = seq // 2, head // 2

    def per_device(cache, qn, qr, se, off, uk, uv, go):
        own, width = cache.shape
        half = own // 2
        keys = own * seq
        queries = qn.shape[0]
        heads = qn.shape[1] // NOPE
        rows = heads * queries
        vm = pltpu.VMEM
        dma = pltpu.SemaphoreType.DMA
        vspec = pl.BlockSpec(memory_space=pltpu.VMEM)
        sspec = pl.BlockSpec(memory_space=pltpu.SMEM)
        return pl.pallas_call(
            functools.partial(kernel, nz, nx),
            out_shape=(
                jax.ShapeDtypeStruct(cache.shape, BF16),
                jax.ShapeDtypeStruct(qn.shape, BF16),
                jax.ShapeDtypeStruct(qr.shape, BF16),
            ),
            in_specs=[vspec, vspec, vspec, vspec, sspec, vspec, vspec, vspec],
            out_specs=(vspec, vspec, vspec),
            scratch_shapes=[
                vm((keys, width), BF16), vm((width, keys), BF16),
                vm((width, rows), BF16), vm((rows, width), BF16),
                vm((LATENT, rows), BF16), vm((rows, LATENT), BF16),
                vm((heads * NOPE, LATENT), BF16),
                vm((keys, rows), F32), vm((keys, rows), F32),
                vm((keys, rows), BF16), vm((keys, rows), BF16),
                vm((8, rows), F32), vm((keys, width), F32),
                vm((nz, 2, half, width), BF16), vm((nz, 2, half, width), BF16),
                vm((nz, half, width), BF16), vm((nz, half, width), BF16),
                vm((nz, half, width), BF16), vm((nz, half, width), BF16),
                vm((half, width), BF16), vm((nx, half, width), BF16),
                vm((half, width), BF16), vm((half, width), BF16),
                dma((nz,)), dma((nz,)), dma((2 * nz,)), dma((2 * seq,)),
                dma((nz,)), dma((nz,)), dma((nz,)), dma((nz,)),
                dma((nz,)), dma((nz,)), dma((nx,)), dma((nx,)), dma((1,)), dma((1,)),
            ],
            compiler_params=pltpu.CompilerParams(
                collective_id=0, has_side_effects=True, vmem_limit_bytes=60 * 1024 * 1024
            ),
        )(cache, qn, qr, se.reshape(1, -1), off, uk, uv, go)

    in_specs = (
        P("seq", None), P("seq", "head"), P("seq", "head"), P("seq"), P("seq"),
        P(None, "head"), P(None, "head"), P("seq", "head"),
    )
    out_specs = (P("seq", None), P("seq", "head"), P("seq", "head"))
    return jax.shard_map(
        per_device, mesh=mesh, in_specs=in_specs, out_specs=out_specs, check_vma=False
    )
```

profile of v0, /device:TPU:0, one launch (start us, length us, event | category | flops | bytes accessed | tf_op | source)
XLA Modules:
  0.0 54.3 jit_solution(7340278488112406580)
XLA Ops:
  0.6 1.7 %copy.11.cache_ref = bf16[128,576]{1,0:T(8,128)(2,1)} copy(bf16[128,576]{0,1:T(8,128)(2,1)} %param.8) | data formatting | bytes 294912 | tf_op args[0]
  2.3 48.5 %shard_map.103 = (bf16[128,576]{1,0:T(8,128)(2,1)}, bf16[128,1024]{1,0:T(8,128)(2,1)}, bf16[128,512]{1,0:T(8,128)(2,1)}) custom-call(bf16[128,576]{1,0:T(8,128)(2,1)} %copy.11.cache_ref, bf16[128,1024]{1,0:T(8,128)(2,1)} %qn_ref.1, bf16[128,512]{1,0:T(8,128)(2,1)} %qr_ref.1, s32[1,128]{1,0:T(1,128)} %bitcast.1, s32[2]{0:T(128)} %off_ref.1, ...), custom_call_target="tpu_custom_call" | custom-call | tf_op jit(solution)/shard_map/pallas_call | solution.py:292
  50.9 0.0 copy-start
  50.9 1.7 %copy.12 = bf16[128,576]{0,1:T(8,128)(2,1)} copy(bf16[128,576]{1,0:T(8,128)(2,1)} %get-tuple-element.3) | data formatting | bytes 294912 | tf_op jit(solution)/shard_map/pallas_call | solution.py:292
  52.6 0.0 copy-done
  52.7 0.0 copy-start.1
  52.7 0.7 %copy.15 = bf16[128,1024]{1,0:T(8,128)(2,1)} copy(bf16[128,1024]{1,0:T(8,128)(2,1)S(1)} %copy-done) | data formatting | bytes 524288
  53.4 0.3 copy-done.1
  53.7 0.7 %copy.16 = bf16[128,512]{1,0:T(8,128)(2,1)} copy(bf16[128,512]{1,0:T(8,128)(2,1)S(1)} %copy-done.1) | data formatting | bytes 262144
Async XLA Ops:
  50.9 1.8 %copy-start = (bf16[128,1024]{1,0:T(8,128)(2,1)S(1)}, bf16[128,1024]{1,0:T(8,128)(2,1)}, u32[]{:S(2)}) copy-start(bf16[128,1024]{1,0:T(8,128)(2,1)} %get-tuple-element.10) | copy-start | bytes 786436
  52.7 1.0 %copy-start.1 = (bf16[128,512]{1,0:T(8,128)(2,1)S(1)}, bf16[128,512]{1,0:T(8,128)(2,1)}, u32[]{:S(2)}) copy-start(bf16[128,512]{1,0:T(8,128)(2,1)} %get-tuple-element.11) | copy-start | bytes 393220
where the time goes:
time: 54.5 us; the launch traced here: 54.3 us
  Pallas kernels  48.5 us (89%)
  local copies, waits for them, and re-layouts  5.11 us (9%)
  between operations  0.65 us (1%)
    pallas_call x1, Pallas kernels, per_device(): pl.pallas_call(functools.partial(kernel, nz, nx), out_shape=(jax.ShapeDty...  48.5 us
    unnamed x7, local copies, waits for them, and re-layouts  3.37 us
    pallas_call x1, local copies, waits for them, and re-layouts, per_device(): pl.pallas_call(functools.partial(kernel, nz, nx), out_shape=(jax.ShapeDty...  1.74 us

commit v1 on v0

v1 whole, which is shorter than its diff:
```python
import functools
import math

import jax
import jax.numpy as jnp
from jax import lax
from jax.experimental import pallas as pl
from jax.experimental.pallas import tpu as pltpu
from jax.sharding import PartitionSpec as P

LATENT = 512
ROPE = 64
NOPE = 128
QBLOCK = 64
MESH = pl.DeviceIdType.MESH
BF16 = jnp.bfloat16
F32 = jnp.float32
NEG = -1e30


def dot(a, b):
    return jnp.dot(a, b, preferred_element_type=F32)


def dot_nt(a, b):
    return lax.dot_general(a, b, (((1,), (1,)), ((), ())), preferred_element_type=F32)


def flip(v, k):
    bit = 1
    while bit <= k:
        if k & bit:
            v = v + bit - 2 * bit * lax.rem(v // bit, 2)
        bit *= 2
    return v


def kernel(
    nz, nx,
    cache_ref, qn_ref, qr_ref, se_ref, off_ref, uk_ref, uv_ref, go_ref,
    dc_ref, dqn_ref, dqr_ref,
    land, full, cT, extT, ext, backT, back, upkT, S, dP, pT, dsT, mx, D,
    csnd, crcv, psnd, prcv, zsnd, zrcv, wsnd, wrcv, fin,
    g_send, g_recv, c_send, c_recv, p_send, p_recv, z_send, z_recv,
    w_send, w_recv, f_send, f_recv,
):
    width, own = cache_ref.shape
    hwide, qwide = width // 2, width // 4
    half, quarter = own // 2, own // 4
    pair = 2 * own
    queries = qn_ref.shape[0]
    heads = qn_ref.shape[1] // NOPE
    rows = heads * queries
    scale = (NOPE + ROPE) ** (-0.5)
    s_me = lax.axis_index("seq")
    h_me = lax.axis_index("head")
    z, y = s_me // 2, lax.rem(s_me, 2)
    x, core = h_me // 2, lax.rem(h_me, 2)
    xg, xp = x // 2, lax.rem(x, 2)
    oy, oc, oxp = 1 - y, 1 - core, 1 - xp
    ngroups = nx // 2

    def at(zz, yy, xx, cc):
        return (zz * 2 + yy, xx * 2 + cc)

    xo = xg * 2 + oxp
    zs = [flip(z, k) for k in range(nz)]
    z_devs = [at(zz, y, x, core) for zz in zs]
    y_dev = at(z, oy, x, core)
    x_dev = at(z, y, xo, core)
    xy_dev = at(z, oy, xo, core)
    c_dev = at(z, y, x, oc)
    xc_dev = at(z, y, xo, oc)
    xgs = [lax.rem(xg + k, ngroups) for k in range(ngroups)]
    g_devs = [at(z, y, g * 2 + xp, core) for g in xgs]

    barrier = pltpu.get_barrier_semaphore()
    peers = z_devs[1:] + [y_dev, x_dev, xy_dev, c_dev, xc_dev] + g_devs[1:]
    for dev in peers:
        pl.semaphore_signal(barrier, inc=1, device_id=dev, device_id_type=MESH)
    pl.semaphore_wait(barrier, len(peers))

    def remote(src, dst, send, recv, dev):
        return pltpu.make_async_remote_copy(
            src_ref=src, dst_ref=dst, send_sem=send, recv_sem=recv,
            device_id=dev, device_id_type=MESH,
        )

    sends = []

    def go(copy):
        copy.start()
        sends.append(copy)

    counter = [0]

    def part(cc, xx):
        return pl.ds(pl.multiple_of(cc * hwide + xx * qwide, 16), qwide)

    def whole(cc):
        return pl.ds(pl.multiple_of(cc * hwide, 16), hwide)

    def gather(src, blk, rs, slot, dev):
        i = counter[0]
        counter[0] += 1
        go(remote(src, land.at[blk, rs], g_send.at[i], g_recv.at[blk * 4 + slot], dev))

    def arrived(blk, rs, slot):
        remote(
            land.at[blk, rs], land.at[blk, rs], g_send.at[0], g_recv.at[blk * 4 + slot], c_dev
        ).wait_recv()

    mine = part(core, xp)
    for k in range(1, nz):
        gather(cache_ref.at[mine], s_me, mine, 0, z_devs[k])
    gather(cache_ref.at[whole(core)], s_me, whole(core), 0, y_dev)

    land[s_me] = cache_ref[...]

    def block(k, yy):
        return zs[k] * 2 + yy

    def e_own():
        blk = block(0, oy)
        arrived(blk, whole(core), 0)
        gather(land.at[blk, whole(core)], blk, whole(core), 2, c_dev)

    def e_z(k):
        blk = block(k, y)
        arrived(blk, mine, 0)
        gather(land.at[blk, mine], blk, mine, 0, y_dev)
        gather(land.at[blk, mine], blk, mine, 1, x_dev)

    def e_y(k):
        blk = block(k, oy)
        arrived(blk, mine, 0)
        gather(land.at[blk, mine], blk, mine, 1, x_dev)

    def e_x(k, yy):
        blk = block(k, yy)
        arrived(blk, part(core, oxp), 1)
        gather(land.at[blk, whole(core)], blk, whole(core), 2, c_dev)

    def e_c(k):
        if k:
            arrived(block(k, y), whole(oc), 2)
        arrived(block(k, oy), whole(oc), 2)

    factor = jnp.exp2(se_ref[...].astype(F32))
    lane = lax.broadcasted_iota(jnp.int32, (1, queries), 1)
    pos = jnp.zeros((1, queries), jnp.int32)
    for b in range(queries // QBLOCK):
        inside = (lane >= b * QBLOCK) & (lane < (b + 1) * QBLOCK)
        pos = jnp.where(inside, off_ref[b] + lane - b * QBLOCK, pos)

    for h in range(heads):
        cols = slice(h * NOPE, (h + 1) * NOPE)
        qs = slice(h * queries, (h + 1) * queries)
        w = uk_ref[:, cols]
        a = (dot_nt(w, qn_ref[:, cols]) * factor).astype(BF16)
        extT[0:LATENT, qs] = a
        ext[qs, 0:LATENT] = a.T
        upkT[cols, :] = w.T
        g = dot_nt(uv_ref[:, cols], go_ref[:, cols]).astype(BF16)
        backT[:, qs] = g
        back[qs, :] = g.T
    for h in range(0, heads, 2):
        r = (qr_ref[:, h * ROPE : (h + 2) * ROPE].astype(F32).T * factor).astype(BF16)
        for i in range(2):
            p = r[i * ROPE : (i + 1) * ROPE, :]
            qs = slice((h + i) * queries, (h + i + 1) * queries)
            extT[LATENT:width, qs] = p
            ext[qs, LATENT:width] = p.astype(F32).T.astype(BF16)
    mx[...] = jnp.full(mx.shape, NEG, F32)

    tile = 2 * queries
    pos2 = jnp.concatenate([pos, pos], axis=1)
    tiles = rows // tile

    def base_of(k):
        return pl.multiple_of(zs[k] * pair, pair)

    def turn(k):
        for yy in range(2):
            at_col = pl.ds(pl.multiple_of((zs[k] * 2 + yy) * own, own), own)
            b = land[zs[k] * 2 + yy]
            cT[:, at_col] = b
            full[at_col, :] = b.T

    def scores(k, t):
        base = base_of(k)
        c = full[pl.ds(base, pair), :]
        key = base + lax.broadcasted_iota(jnp.int32, (pair, tile), 0)
        seen = key <= pos2
        ls = slice(t * tile, (t + 1) * tile)
        s = dot(c, extT[:, ls]) * (scale * math.log2(math.e))
        s = jnp.where(seen, s, NEG)
        S[pl.ds(base, pair), ls] = s
        mx[:, ls] = jnp.maximum(mx[:, ls], jnp.max(s.reshape(pair // 8, 8, tile), axis=0))
        dP[pl.ds(base, pair), ls] = dot(c[:, :LATENT], backT[:, ls])

    events = [functools.partial(e_z, 1), e_own]
    events += [functools.partial(e_z, k) for k in range(2, nz)]
    work = []
    for k in range(1, nz):
        events += [functools.partial(e_y, k), functools.partial(e_x, k, y)]
    late = [functools.partial(e_x, k, oy) for k in range(1, nz)]

    def pieces(k):
        def first():
            e_c(k)
            turn(k)
            scores(k, 0)

        return [first] + [functools.partial(scores, k, t) for t in range(1, tiles)]

    for e in events[:nz]:
        e()
    work = pieces(0)
    rest = events[nz:]
    while rest:
        rest.pop(0)()
        if work:
            work.pop(0)()
    for w_ in work:
        w_()
    for k in range(1, nz):
        late.pop(0)()
        if k > 1:
            for p in pieces(k - 1):
                p()
    for p in pieces(nz - 1):
        p()

    keys = full.shape[0]
    chunk = own

    def soften(h, carry):
        ls = pl.ds(pl.multiple_of(h * queries, queries), queries)
        top = jnp.max(mx[:, ls], axis=0, keepdims=True)
        tot = jnp.zeros((8, queries), F32)
        dl = jnp.zeros((8, queries), F32)
        for i in range(keys // chunk):
            rs = slice(i * chunk, (i + 1) * chunk)
            p = jnp.exp2(S[rs, ls] - top)
            S[rs, ls] = p
            tot = tot + jnp.sum(p.reshape(chunk // 8, 8, queries), axis=0)
            dl = dl + jnp.sum((p * dP[rs, ls]).reshape(chunk // 8, 8, queries), axis=0)
        inv = 1.0 / jnp.sum(tot, axis=0, keepdims=True)
        delta = jnp.sum(dl, axis=0, keepdims=True) * inv
        for i in range(keys // chunk):
            rs = slice(i * chunk, (i + 1) * chunk)
            pr = S[rs, ls] * inv
            pT[rs, ls] = pr.astype(BF16)
            dsT[rs, ls] = (pr * (dP[rs, ls] - delta) * scale).astype(BF16)
        return carry

    lax.fori_loop(0, heads, soften, 0)

    def span(zz, yy, cc, xx=None):
        start = (zz * 2 + yy) * own + cc * half
        if xx is None:
            return pl.ds(pl.multiple_of(start, half), half)
        return pl.ds(pl.multiple_of(start + xx * quarter, quarter), quarter)

    def core_copy(k):
        return remote(csnd.at[k], crcv.at[k], c_send.at[k], c_recv.at[k], c_dev)

    plane = [(oy, xp, y_dev), (y, oxp, x_dev), (oy, oxp, xy_dev)]

    def plane_copy(k, i):
        return remote(
            psnd.at[k, i], prcv.at[k, i], p_send.at[k * 3 + i], p_recv.at[k * 3 + i], plane[i][2]
        )

    def z_copy(k):
        return remote(zsnd.at[k], zrcv.at[k], z_send.at[k], z_recv.at[k], z_devs[k])

    def step_d(k):
        rs = pl.ds(base_of(k), pair)
        ds, pb = dsT[rs, :], pT[rs, :]
        D[rs, 0:LATENT] = dot(ds, ext[:, 0:LATENT]) + dot(pb, back[...])
        D[rs, LATENT:width] = dot(ds, ext[:, LATENT:width])
        for yy in range(2):
            csnd[k, yy] = D[span(zs[k], yy, oc), :].astype(BF16)
        go(core_copy(k))

    def quarter_of(k, yy, xx):
        rs = pl.ds(pl.multiple_of(xx * quarter, quarter), quarter)
        return D[span(zs[k], yy, core, xx), :] + crcv[k, yy, rs, :].astype(F32)

    def step_e(k):
        core_copy(k).wait_recv()
        for i in (2, 0, 1):
            yy, xx, _ = plane[i]
            psnd[k, i] = quarter_of(k, yy, xx).astype(BF16)
            go(plane_copy(k, i))

    def step_f(k):
        u = quarter_of(k, y, xp)
        for i in range(3):
            plane_copy(k, i).wait_recv()
            u = u + prcv[k, i].astype(F32)
        if k:
            zsnd[k] = u.astype(BF16)
            go(z_copy(k))
        return u

    def grads(h):
        g = dot(cT[...], dsT[:, h * queries : (h + 2) * queries])
        lo = g[0:LATENT].astype(BF16)
        hi = g[LATENT:width]
        ropes = []
        for i in range(2):
            qs = slice(i * queries, (i + 1) * queries)
            cols = slice((h + i) * NOPE, (h + i + 1) * NOPE)
            d = dot(upkT[cols, :], lo[:, qs]) * factor
            dqn_ref[:, cols] = d.T.astype(BF16)
            ropes.append(hi[:, qs] * factor)
        dqr_ref[:, h * ROPE : (h + 2) * ROPE] = jnp.concatenate(ropes, axis=0).T.astype(BF16)

    order = list(range(nz - 1, -1, -1))
    todo = list(range(0, heads, 2))
    ready_e, ready_f = [], []
    for i, k in enumerate(order):
        step_d(k)
        if i > 0:
            step_e(order[i - 1])
        if i > 2:
            step_f(order[i - 3])
    grads(todo.pop(0))
    step_e(order[-1])
    for k in order[max(0, nz - 3) : -1]:
        step_f(k)
        if todo:
            grads(todo.pop(0))
    while todo:
        grads(todo.pop(0))
    v = step_f(0)
    for k in range(1, nz):
        z_copy(k).wait_recv()
        v = v + zrcv[k].astype(F32)
    if ngroups > 1:
        wsnd[...] = v.astype(BF16)
        for k in range(1, ngroups):
            go(remote(wsnd, wrcv.at[xg], w_send.at[k], w_recv.at[xg], g_devs[k]))
        wrcv[xg] = v.astype(BF16)
        for k in range(1, ngroups):
            remote(wsnd, wrcv.at[xgs[k]], w_send.at[k], w_recv.at[xgs[k]], g_devs[k]).wait_recv()
        v = wrcv[0].astype(F32)
        for i in range(1, ngroups):
            v = v + wrcv[i].astype(F32)
    here = pl.ds(pl.multiple_of(core * half + xp * quarter, quarter), quarter)
    fin[here, :] = v.astype(BF16)
    last = [(core, oxp, x_dev), (oc, oxp, xc_dev), (oc, xp, c_dev)]
    for i, (_, _, dev) in enumerate(last):
        go(remote(fin.at[here], fin.at[here], f_send.at[i], f_recv.at[i], dev))
    for i, (cc, xx, dev) in enumerate(last):
        there = pl.ds(pl.multiple_of(cc * half + xx * quarter, quarter), quarter)
        remote(fin.at[there], fin.at[there], f_send.at[i], f_recv.at[i], dev).wait_recv()
    dc_ref[...] = fin[...].T
    for copy in sends:
        copy.wait_send()


def finish(a, b, c, oa, ob, oc, sem):
    copies = [
        pltpu.make_async_copy(src, dst, sem.at[i])
        for i, (src, dst) in enumerate(((b, ob), (a, oa), (c, oc)))
    ]
    for copy in copies:
        copy.start()
    for copy in copies:
        copy.wait()


def solution(mesh):
    seq, head = mesh.shape["seq"], mesh.shape["head"]
    nz, nx = seq // 2, head // 2

    def per_device(cache, qn, qr, se, off, uk, uv, go):
        own, width = cache.shape
        half, quarter = own // 2, own // 4
        keys = own * seq
        queries = qn.shape[0]
        heads = qn.shape[1] // NOPE
        rows = heads * queries
        vm = pltpu.VMEM
        dma = pltpu.SemaphoreType.DMA
        vspec = pl.BlockSpec(memory_space=pltpu.VMEM)
        sspec = pl.BlockSpec(memory_space=pltpu.SMEM)
        hspec = pl.BlockSpec(memory_space=pl.ANY)
        shapes = ((width, own), qn.shape, qr.shape)
        out = pl.pallas_call(
            functools.partial(kernel, nz, nx),
            out_shape=tuple(vm(s, BF16) for s in shapes),
            in_specs=[vspec, vspec, vspec, vspec, sspec, vspec, vspec, vspec],
            out_specs=(vspec, vspec, vspec),
            scratch_shapes=[
                vm((seq, width, own), BF16), vm((keys, width), BF16), vm((width, keys), BF16),
                vm((width, rows), BF16), vm((rows, width), BF16),
                vm((LATENT, rows), BF16), vm((rows, LATENT), BF16),
                vm((heads * NOPE, LATENT), BF16),
                vm((keys, rows), F32), vm((keys, rows), F32),
                vm((keys, rows), BF16), vm((keys, rows), BF16),
                vm((8, rows), F32), vm((keys, width), F32),
                vm((nz, 2, half, width), BF16), vm((nz, 2, half, width), BF16),
                vm((nz, 3, quarter, width), BF16), vm((nz, 3, quarter, width), BF16),
                vm((nz, quarter, width), BF16), vm((nz, quarter, width), BF16),
                vm((quarter, width), BF16), vm((nx // 2, quarter, width), BF16),
                vm((own, width), BF16),
                dma((8 * nz,)), dma((4 * seq,)), dma((nz,)), dma((nz,)),
                dma((3 * nz,)), dma((3 * nz,)), dma((nz,)), dma((nz,)),
                dma((nx // 2,)), dma((nx // 2,)), dma((3,)), dma((3,)),
            ],
            compiler_params=pltpu.CompilerParams(
                collective_id=0, has_side_effects=True, vmem_limit_bytes=58 * 1024 * 1024
            ),
        )(cache.T, qn, qr, se.reshape(1, -1), off, uk, uv, go)
        dc, dqn, dqr = pl.pallas_call(
            finish,
            out_shape=tuple(jax.ShapeDtypeStruct(s, BF16) for s in shapes),
            in_specs=[vspec] * 3,
            out_specs=(hspec,) * 3,
            scratch_shapes=[dma((3,))],
            compiler_params=pltpu.CompilerParams(vmem_limit_bytes=1024 * 1024),
        )(*out)
        return dc.T, dqn, dqr

    in_specs = (
        P("seq", None), P("seq", "head"), P("seq", "head"), P("seq"), P("seq"),
        P(None, "head"), P(None, "head"), P("seq", "head"),
    )
    out_specs = (P("seq", None), P("seq", "head"), P("seq", "head"))
    return jax.shard_map(
        per_device, mesh=mesh, in_specs=in_specs, out_specs=out_specs, check_vma=False
    )
```

time: 54.5 us -> 42.6 us (0.78)
  Pallas kernels: 48.5 us -> 41.8 us
  local copies, waits for them, and re-layouts: 5.11 us -> 0 us
    pallas_call x1 -> x2, Pallas kernels: 48.5 us -> 41.8 us  [the longest x1 41 us: per_device(): pl.pallas_call(functools.partial(kernel, nz, nx), out_shape=tuple((vm(s,...]
    unnamed x7 -> x0, local copies, waits for them, and re-layouts: 3.37 us -> none
    pallas_call x1 -> x0, local copies, waits for them, and re-layouts: 1.74 us -> none  [per_device(): pl.pallas_call(functools.partial(kernel, nz, nx), out_shape=(jax.ShapeDty...]
where the time goes in v1:
time: 42.6 us; the launch traced here: 42.5 us
  Pallas kernels  41.8 us (98%)
  between operations  0.64 us (2%)
    pallas_call x1, Pallas kernels, per_device(): pl.pallas_call(functools.partial(kernel, nz, nx), out_shape=tuple((vm(s,...  41 us

profile of v1, /device:TPU:0, one launch (start us, length us, event | category | flops | bytes accessed | tf_op | source)
XLA Modules:
  0.0 42.5 jit_solution(2292271878946560566)
XLA Ops:
  0.6 41.0 %shard_map.103 = (bf16[576,128]{1,0:T(8,128)(2,1)S(1)}, bf16[128,1024]{1,0:T(8,128)(2,1)S(1)}, bf16[128,512]{1,0:T(8,128)(2,1)S(1)}) custom-call(bf16[576,128]{1,0:T(8,128)(2,1)} %bitcast.3, bf16[128,1024]{1,0:T(8,128)(2,1)} %qn_ref.1, bf16[128,512]{1,0:T(8,128)(2,1)} %qr_ref.1, s32[1,128]{1,0:T(1,128)} %bitcast.4, s32[2]{0:T(128)} %off_ref.1, ...), custom_call_target="tpu_custom_call" | custom-call | tf_op jit(solution)/shard_map/pallas_call | solution.py:394
  41.6 0.8 %shard_map.104 = (bf16[576,128]{1,0:T(8,128)(2,1)}, bf16[128,1024]{1,0:T(8,128)(2,1)}, bf16[128,512]{1,0:T(8,128)(2,1)}) custom-call(bf16[576,128]{1,0:T(8,128)(2,1)S(1)} %get-tuple-element.9.a, bf16[128,1024]{1,0:T(8,128)(2,1)S(1)} %get-tuple-element.10.b, bf16[128,512]{1,0:T(8,128)(2,1)S(1)} %get-tuple-element.11.c), custom_call_target="tpu_custom_call" | custom-call | tf_op jit(solution)/shard_map/pallas_call | solution.py:420

commit v2 on v1

v2 whole, which is shorter than its diff:
```python
import functools
import math

import jax
import jax.numpy as jnp
from jax import lax
from jax.experimental import pallas as pl
from jax.experimental.pallas import tpu as pltpu
from jax.sharding import PartitionSpec as P

LATENT = 512
ROPE = 64
NOPE = 128
QBLOCK = 64
MESH = pl.DeviceIdType.MESH
BF16 = jnp.bfloat16
F32 = jnp.float32
NEG = -1e30


def dot(a, b):
    return jnp.dot(a, b, preferred_element_type=F32)


def dot_nt(a, b):
    return lax.dot_general(a, b, (((1,), (1,)), ((), ())), preferred_element_type=F32)


def flip(v, k):
    bit = 1
    while bit <= k:
        if k & bit:
            v = v + bit - 2 * bit * lax.rem(v // bit, 2)
        bit *= 2
    return v


def kernel(
    nz, nx,
    cache_hbm, qn_hbm, qr_hbm, se_hbm, off_hbm, uk_hbm, uv_hbm, go_hbm,
    dc_ref, dqn_ref, dqr_ref,
    cache_ref, qn_ref, qr_ref, se_ref, off_ref, uk_ref, uv_ref, go_ref,
    land, full, cT, extT, ext, backT, back, upkT, S, dP, pT, dsT, mx, tot, dl, D,
    csnd, crcv, psnd, prcv, zsnd, zrcv, wsnd, wrcv, fin,
    in_sem, g_send, g_recv, c_send, c_recv, p_send, p_recv, z_send, z_recv,
    w_send, w_recv, f_send, f_recv,
):
    width, own = cache_ref.shape
    hwide, qwide = width // 2, width // 4
    half, quarter = own // 2, own // 4
    pair = 2 * own
    queries = qn_ref.shape[0]
    heads = qn_ref.shape[1] // NOPE
    rows = heads * queries
    scale = (NOPE + ROPE) ** (-0.5)
    s_me = lax.axis_index("seq")
    h_me = lax.axis_index("head")
    z, y = s_me // 2, lax.rem(s_me, 2)
    x, core = h_me // 2, lax.rem(h_me, 2)
    xg, xp = x // 2, lax.rem(x, 2)
    oy, oc, oxp = 1 - y, 1 - core, 1 - xp
    ngroups = nx // 2

    loads = [
        pltpu.make_async_copy(src, dst, in_sem.at[i])
        for i, (src, dst) in enumerate((
            (cache_hbm, cache_ref), (se_hbm, se_ref), (off_hbm, off_ref), (qn_hbm, qn_ref),
            (uk_hbm, uk_ref), (go_hbm, go_ref), (uv_hbm, uv_ref), (qr_hbm, qr_ref),
        ))
    ]
    loads[0].start()

    def at(zz, yy, xx, cc):
        return (zz * 2 + yy, xx * 2 + cc)

    xo = xg * 2 + oxp
    zs = [flip(z, k) for k in range(nz)]
    z_devs = [at(zz, y, x, core) for zz in zs]
    y_dev = at(z, oy, x, core)
    x_dev = at(z, y, xo, core)
    xy_dev = at(z, oy, xo, core)
    c_dev = at(z, y, x, oc)
    xc_dev = at(z, y, xo, oc)
    xgs = [lax.rem(xg + k, ngroups) for k in range(ngroups)]
    g_devs = [at(z, y, g * 2 + xp, core) for g in xgs]

    barrier = pltpu.get_barrier_semaphore()
    peers = z_devs[1:] + [y_dev, x_dev, xy_dev, c_dev, xc_dev] + g_devs[1:]
    for dev in peers:
        pl.semaphore_signal(barrier, inc=1, device_id=dev, device_id_type=MESH)
    for load in loads[1:]:
        load.start()
    loads[0].wait()
    pl.semaphore_wait(barrier, len(peers))

    def remote(src, dst, send, recv, dev):
        return pltpu.make_async_remote_copy(
            src_ref=src, dst_ref=dst, send_sem=send, recv_sem=recv,
            device_id=dev, device_id_type=MESH,
        )

    sends = []

    def go(copy):
        copy.start()
        sends.append(copy)

    counter = [0]

    def part(cc, xx):
        return pl.ds(pl.multiple_of(cc * hwide + xx * qwide, 16), qwide)

    def whole(cc):
        return pl.ds(pl.multiple_of(cc * hwide, 16), hwide)

    mine, theirs = part(core, xp), part(core, oxp)

    def gather(src, k, yy, rs, slot, dev):
        i = counter[0]
        counter[0] += 1
        blk = k * 2 + yy
        go(remote(src, land.at[blk, rs], g_send.at[i], g_recv.at[blk * 4 + slot], dev))

    def pass_on(k, yy, rs, slot, dev):
        gather(land.at[k * 2 + yy, rs], k, yy, rs, slot, dev)

    def arrived(k, yy, rs, slot):
        blk = k * 2 + yy
        remote(
            land.at[blk, rs], land.at[blk, rs], g_send.at[0], g_recv.at[blk * 4 + slot], c_dev
        ).wait_recv()

    for k in list(range(1, nz)):
        gather(cache_ref.at[mine], k, y, mine, 0, z_devs[k])
    gather(cache_ref.at[whole(core)], 0, y, whole(core), 0, y_dev)
    land[y] = cache_ref[...]

    def e_own():
        arrived(0, oy, whole(core), 0)
        pass_on(0, oy, whole(core), 2, c_dev)

    def e_z(k):
        arrived(k, y, mine, 0)
        pass_on(k, y, mine, 1, x_dev)
        pass_on(k, y, mine, 0, y_dev)
        pass_on(k, y, mine, 1, xy_dev)

    def e_h(k):
        arrived(k, y, theirs, 1)
        pass_on(k, y, whole(core), 2, c_dev)
        arrived(k, oy, mine, 0)
        arrived(k, oy, theirs, 1)
        pass_on(k, oy, whole(core), 2, c_dev)

    def e_c(k):
        if k:
            arrived(k, y, whole(oc), 2)
        arrived(k, oy, whole(oc), 2)

    loads[1].wait()
    loads[2].wait()
    factor = jnp.exp2(se_ref[...].astype(F32))
    lane = lax.broadcasted_iota(jnp.int32, (1, queries), 1)
    pos = jnp.zeros((1, queries), jnp.int32)
    for b in range(queries // QBLOCK):
        inside = (lane >= b * QBLOCK) & (lane < (b + 1) * QBLOCK)
        pos = jnp.where(inside, off_ref[b] + lane - b * QBLOCK, pos)
    for load in loads[3:]:
        load.wait()

    for h in range(heads):
        cols = slice(h * NOPE, (h + 1) * NOPE)
        qs = slice(h * queries, (h + 1) * queries)
        w = uk_ref[:, cols]
        a = (dot_nt(w, qn_ref[:, cols]) * factor).astype(BF16)
        extT[0:LATENT, qs] = a
        ext[qs, 0:LATENT] = a.T
        upkT[cols, :] = w.T
        g = dot_nt(uv_ref[:, cols], go_ref[:, cols]).astype(BF16)
        backT[:, qs] = g
        back[qs, :] = g.T
    for h in range(0, heads, 2):
        r = (qr_ref[:, h * ROPE : (h + 2) * ROPE].astype(F32).T * factor).astype(BF16)
        for i in range(2):
            p = r[i * ROPE : (i + 1) * ROPE, :]
            qs = slice((h + i) * queries, (h + i + 1) * queries)
            extT[LATENT:width, qs] = p
            ext[qs, LATENT:width] = p.astype(F32).T.astype(BF16)

    tile = 2 * queries
    pos2 = jnp.concatenate([pos, pos], axis=1)
    tiles = rows // tile

    def turn(k):
        for yy in range(2):
            cols = slice(k * pair + yy * own, k * pair + (yy + 1) * own)
            b = land[k * 2 + yy]
            cT[:, cols] = b
            full[cols, :] = b.T

    def scores(k, first, last):
        rs = slice(k * pair, (k + 1) * pair)
        c = full[rs, :]
        key = zs[k] * pair + lax.broadcasted_iota(jnp.int32, (pair, tile), 0)
        seen = key <= pos2
        for t in range(first, last):
            ls = slice(t * tile, (t + 1) * tile)
            s = dot(c, extT[:, ls]) * (scale * math.log2(math.e))
            s = jnp.where(seen, s, NEG)
            S[rs, ls] = s
            mx[k, :, ls] = jnp.max(s.reshape(pair // 8, 8, tile), axis=0)
            dP[rs, ls] = dot(c[:, :LATENT], backT[:, ls])

    def soft(k, t):
        ls = slice(t * tile, (t + 1) * tile)
        top = jnp.max(mx[k, :, ls], axis=0, keepdims=True)
        t8 = jnp.zeros((8, tile), F32)
        d8 = jnp.zeros((8, tile), F32)
        for i in range(2):
            n = pair // 2
            rs = slice(k * pair + i * n, k * pair + (i + 1) * n)
            p = jnp.exp2(S[rs, ls] - top)
            S[rs, ls] = p
            t8 = t8 + jnp.sum(p.reshape(n // 8, 8, tile), axis=0)
            d8 = d8 + jnp.sum((p * dP[rs, ls]).reshape(n // 8, 8, tile), axis=0)
        tot[k, :, ls] = t8
        dl[k, :, ls] = d8

    def both(k, first, last):
        for t in range(first, last):
            scores(k, t, t + 1)
            if t > first:
                soft(k, t - 1)
        soft(k, last - 1)

    ks = list(range(1, nz))
    e_z(ks[0])
    e_own()
    for k in ks[1:]:
        e_z(k)
    e_c(0)
    turn(0)
    both(0, 0, tiles)
    e_h(ks[0])
    for i, k in enumerate(ks):
        for kk in ks[i + 1 : i + 2]:
            e_h(kk)
        e_c(k)
        turn(k)
        both(k, 0, tiles)
    tops = [jnp.max(mx[k], axis=0, keepdims=True) for k in range(nz)]
    top = functools.reduce(jnp.maximum, tops)
    parts = [jnp.exp2(t - top) for t in tops]
    total = sum(p * jnp.sum(tot[k], axis=0, keepdims=True) for k, p in enumerate(parts))
    delta = sum(p * jnp.sum(dl[k], axis=0, keepdims=True) for k, p in enumerate(parts))
    inv = 1.0 / total
    delta = delta * inv

    def settle(k, i):
        f = parts[k] * inv
        for h in range(heads):
            ls = slice(h * queries, (h + 1) * queries)
            rs = slice(k * pair + i * own, k * pair + (i + 1) * own)
            pr = S[rs, ls] * f[:, ls]
            pT[rs, ls] = pr.astype(BF16)
            dsT[rs, ls] = (pr * (dP[rs, ls] - delta[:, ls]) * scale).astype(BF16)

    def step_piece(k, yy):
        rs = slice(k * pair + yy * own, k * pair + (yy + 1) * own)
        ds, pb = dsT[rs, :], pT[rs, :]
        v = dot(ds, ext[:, 0:LATENT]) + dot(pb, back[...])
        t = dot(ds, ext[:, LATENT:width])
        n = quarter // 2
        for c in range(2):
            for xx in range(2):
                r = c * half + xx * quarter
                for j in range(LATENT // 128):
                    cols = slice(j * 128, (j + 1) * 128)
                    D[k, yy, c, xx, j * quarter : (j + 1) * quarter, :] = v[r : r + quarter, cols]
                tail = jnp.concatenate([t[r : r + n], t[r + n : r + quarter]], axis=1)
                D[k, yy, c, xx, LATENT // 128 * quarter :, :] = tail

    def core_copy(k):
        return remote(csnd.at[k], crcv.at[k], c_send.at[k], c_recv.at[k], c_dev)

    plane = [(oy, xp, y_dev), (y, oxp, x_dev), (oy, oxp, xy_dev)]

    def plane_copy(k, i):
        return remote(
            psnd.at[k, i], prcv.at[k, i], p_send.at[k * 3 + i], p_recv.at[k * 3 + i], plane[i][2]
        )

    def z_copy(k):
        return remote(zsnd.at[k], zrcv.at[k], z_send.at[k], z_recv.at[k], z_devs[k])

    def step_d(k, then):
        for yy in range(2):
            step_piece(k, yy)
            if then is not None:
                settle(then, yy)
        for yy in range(2):
            csnd[k, yy] = D[k, yy, oc].astype(BF16)
        go(core_copy(k))

    def chip_sum(k, yy, xx):
        return D[k, yy, core, xx] + crcv[k, yy, xx].astype(F32)

    def step_e(k):
        core_copy(k).wait_recv()
        for i in (2, 0, 1):
            yy, xx, _ = plane[i]
            psnd[k, i] = chip_sum(k, yy, xx).astype(BF16)
            go(plane_copy(k, i))

    def step_f(k):
        u = chip_sum(k, y, xp)
        for i in range(3):
            plane_copy(k, i).wait_recv()
            u = u + prcv[k, i].astype(F32)
        if k:
            zsnd[k] = u.astype(BF16)
            go(z_copy(k))
        return u

    def grad_ext(h):
        cols = slice(h * queries, (h + 2) * queries)
        g = dot(cT[...], dsT[:, cols])
        extT[0:LATENT, cols] = g[0:LATENT].astype(BF16)
        hi = g[LATENT:width]
        ropes = [hi[:, i * queries : (i + 1) * queries] * factor for i in range(2)]
        dqr_ref[:, h * ROPE : (h + 2) * ROPE] = jnp.concatenate(ropes, axis=0).T.astype(BF16)

    def grad_nope(h):
        for i in range(h, h + 2):
            cols = slice(i * NOPE, (i + 1) * NOPE)
            d = dot(upkT[cols, :], extT[0:LATENT, i * queries : (i + 1) * queries]) * factor
            dqn_ref[:, cols] = d.T.astype(BF16)

    todo = [functools.partial(grad_ext, 0)]
    for h in range(2, heads, 2):
        todo += [functools.partial(grad_ext, h), functools.partial(grad_nope, h - 2)]
    todo += [functools.partial(grad_nope, heads - 2)]

    def some(n):
        for _ in range(n):
            if todo:
                todo.pop(0)()

    order = list(range(nz - 1, -1, -1))
    settle(order[0], 0)
    settle(order[0], 1)
    waiting = list(order[:-1])
    for i, k in enumerate(order):
        step_d(k, order[i + 1] if i + 1 < nz else None)
        if i > 0:
            step_e(order[i - 1])
        if i > 3:
            step_f(waiting.pop(0))
    some(1)
    step_e(0)
    for i, k in enumerate(waiting):
        some((1, 1, 1)[i] if i < len((1, 1, 1)) else 0)
        step_f(k)
    some(1)
    v = step_f(0)
    for k in range(nz - 1, 0, -1):
        z_copy(k).wait_recv()
        v = v + zrcv[k].astype(F32)
    if ngroups > 1:
        wsnd[...] = v.astype(BF16)
        for k in range(1, ngroups):
            go(remote(wsnd, wrcv.at[xg], w_send.at[k], w_recv.at[xg], g_devs[k]))
        wrcv[xg] = v.astype(BF16)
        for k in range(1, ngroups):
            remote(wsnd, wrcv.at[xgs[k]], w_send.at[k], w_recv.at[xgs[k]], g_devs[k]).wait_recv()
        v = wrcv[0].astype(F32)
        for i in range(1, ngroups):
            v = v + wrcv[i].astype(F32)
    fin[core * 2 + xp] = v.astype(BF16)
    here = fin.at[core * 2 + xp]
    last = [(core, oxp, x_dev), (oc, oxp, xc_dev), (oc, xp, c_dev)]
    for i, (_, _, dev) in enumerate(last):
        go(remote(here, here, f_send.at[i], f_recv.at[i], dev))
    some(len(todo))
    for copy in sends[: -len(last)]:
        copy.wait_send()
    for i, (cc, xx, dev) in enumerate(last):
        there = fin.at[cc * 2 + xx]
        remote(there, there, f_send.at[i], f_recv.at[i], dev).wait_recv()
    quarters = [fin[i].astype(F32) for i in range(4)]
    for j in range(LATENT // 128):
        rs = slice(j * quarter, (j + 1) * quarter)
        tall = jnp.concatenate([q[rs] for q in quarters], axis=0)
        dc_ref[j * 128 : (j + 1) * 128, :] = tall.T.astype(BF16)
    rs = slice(LATENT // 128 * quarter, quarter * width // 128)
    tails = [q[rs, i * ROPE : (i + 1) * ROPE] for q in quarters for i in range(2)]
    dc_ref[LATENT:width, :] = jnp.concatenate(tails, axis=0).T.astype(BF16)
    for copy in sends[-len(last) :]:
        copy.wait_send()


def finish(a, b, c, oa, ob, oc, sem):
    copies = [
        pltpu.make_async_copy(src, dst, sem.at[i])
        for i, (src, dst) in enumerate(((b, ob), (a, oa), (c, oc)))
    ]
    for copy in copies:
        copy.start()
    for copy in copies:
        copy.wait()


def solution(mesh):
    seq, head = mesh.shape["seq"], mesh.shape["head"]
    nz, nx = seq // 2, head // 2

    def per_device(cache, qn, qr, se, off, uk, uv, go):
        own, width = cache.shape
        keys = own * seq
        prow = own // 4 * width // 128
        queries = qn.shape[0]
        heads = qn.shape[1] // NOPE
        rows = heads * queries
        vm = pltpu.VMEM
        dma = pltpu.SemaphoreType.DMA
        vspec = pl.BlockSpec(memory_space=pltpu.VMEM)
        hspec = pl.BlockSpec(memory_space=pl.ANY)
        shapes = ((width, own), qn.shape, qr.shape)
        out = pl.pallas_call(
            functools.partial(kernel, nz, nx),
            out_shape=tuple(vm(s, BF16) for s in shapes),
            in_specs=[hspec] * 8,
            out_specs=(vspec, vspec, vspec),
            scratch_shapes=[
                vm((width, own), BF16), vm(qn.shape, BF16), vm(qr.shape, BF16),
                vm((1, queries), jnp.int32), pltpu.SMEM(off.shape, jnp.int32),
                vm(uk.shape, BF16), vm(uv.shape, BF16), vm(go.shape, BF16),
                vm((seq, width, own), BF16), vm((keys, width), BF16), vm((width, keys), BF16),
                vm((width, rows), BF16), vm((rows, width), BF16),
                vm((LATENT, rows), BF16), vm((rows, LATENT), BF16),
                vm((heads * NOPE, LATENT), BF16),
                vm((keys, rows), F32), vm((keys, rows), F32),
                vm((keys, rows), BF16), vm((keys, rows), BF16),
                vm((nz, 8, rows), F32), vm((nz, 8, rows), F32), vm((nz, 8, rows), F32),
                vm((nz, 2, 2, 2, prow, 128), F32),
                vm((nz, 2, 2, prow, 128), BF16), vm((nz, 2, 2, prow, 128), BF16),
                vm((nz, 3, prow, 128), BF16), vm((nz, 3, prow, 128), BF16),
                vm((nz, prow, 128), BF16), vm((nz, prow, 128), BF16),
                vm((prow, 128), BF16), vm((nx // 2, prow, 128), BF16),
                vm((4, prow, 128), BF16),
                dma((8,)), dma((6 * nz + 4,)), dma((4 * seq,)), dma((nz,)), dma((nz,)),
                dma((3 * nz,)), dma((3 * nz,)), dma((nz,)), dma((nz,)),
                dma((nx // 2,)), dma((nx // 2,)), dma((3,)), dma((3,)),
            ],
            compiler_params=pltpu.CompilerParams(
                collective_id=0, has_side_effects=True, vmem_limit_bytes=58 * 1024 * 1024
            ),
        )(cache.T, qn, qr, se.reshape(1, -1), off, uk, uv, go)
        dc, dqn, dqr = pl.pallas_call(
            finish,
            out_shape=tuple(jax.ShapeDtypeStruct(s, BF16) for s in shapes),
            in_specs=[vspec] * 3,
            out_specs=(hspec,) * 3,
            scratch_shapes=[dma((3,))],
            compiler_params=pltpu.CompilerParams(vmem_limit_bytes=1024 * 1024),
        )(*out)
        return dc.T, dqn, dqr

    in_specs = (
        P("seq", None), P("seq", "head"), P("seq", "head"), P("seq"), P("seq"),
        P(None, "head"), P(None, "head"), P("seq", "head"),
    )
    out_specs = (P("seq", None), P("seq", "head"), P("seq", "head"))
    return jax.shard_map(
        per_device, mesh=mesh, in_specs=in_specs, out_specs=out_specs, check_vma=False
    )
```

time: 42.6 us -> 36.5 us (0.86)
  Pallas kernels: 41.8 us -> 35.7 us
    pallas_call x1, Pallas kernels: 41 us -> 34.9 us  [per_device(): pl.pallas_call(functools.partial(kernel, nz, nx), out_shape=tuple((vm(s,...]
where the time goes in v2:
time: 36.5 us; the launch traced here: 36.4 us
  Pallas kernels  35.7 us (98%)
  between operations  0.64 us (2%)
    pallas_call x1, Pallas kernels, per_device(): pl.pallas_call(functools.partial(kernel, nz, nx), out_shape=tuple((vm(s,...  34.9 us
    pallas_call x1, Pallas kernels, per_device(): pl.pallas_call(finish, out_shape=tuple((jax.ShapeDtypeStruct(s, BF16) for...  0.82 us

profile of v2, /device:TPU:0, one launch (start us, length us, event | category | flops | bytes accessed | tf_op | source)
XLA Modules:
  0.0 36.4 jit_solution(5190821032482706704)
XLA Ops:
  0.6 34.9 %shard_map.103 = (bf16[576,128]{1,0:T(8,128)(2,1)S(1)}, bf16[128,1024]{1,0:T(8,128)(2,1)S(1)}, bf16[128,512]{1,0:T(8,128)(2,1)S(1)}) custom-call(bf16[576,128]{1,0:T(8,128)(2,1)} %bitcast.3, bf16[128,1024]{1,0:T(8,128)(2,1)} %qn_hbm.1, bf16[128,512]{1,0:T(8,128)(2,1)} %qr_hbm.1, s32[1,128]{1,0:T(1,128)} %bitcast.4, s32[2]{0:T(128)} %off_hbm.1, ...), custom_call_target="tpu_custom_call" | custom-call | tf_op jit(solution)/shard_map/pallas_call | solution.py:429
  35.6 0.8 %shard_map.104 = (bf16[576,128]{1,0:T(8,128)(2,1)}, bf16[128,1024]{1,0:T(8,128)(2,1)}, bf16[128,512]{1,0:T(8,128)(2,1)}) custom-call(bf16[576,128]{1,0:T(8,128)(2,1)S(1)} %get-tuple-element.9.a, bf16[128,1024]{1,0:T(8,128)(2,1)S(1)} %get-tuple-element.10.b, bf16[128,512]{1,0:T(8,128)(2,1)S(1)} %get-tuple-element.11.c), custom_call_target="tpu_custom_call" | custom-call | tf_op jit(solution)/shard_map/pallas_call | solution.py:459

commit v3 on v2

v3 whole, which is shorter than its diff:
```python
import functools
import math

import jax
import jax.numpy as jnp
from jax import lax
from jax.experimental import pallas as pl
from jax.experimental.pallas import tpu as pltpu
from jax.sharding import PartitionSpec as P

LATENT = 512
ROPE = 64
NOPE = 128
QBLOCK = 64
MESH = pl.DeviceIdType.MESH
BF16 = jnp.bfloat16
F32 = jnp.float32
NEG = -1e30


def dot(a, b):
    return jnp.dot(a, b, preferred_element_type=F32)


def dot_nt(a, b):
    return lax.dot_general(a, b, (((1,), (1,)), ((), ())), preferred_element_type=F32)


def flip(v, k):
    bit = 1
    while bit <= k:
        if k & bit:
            v = v + bit - 2 * bit * lax.rem(v // bit, 2)
        bit *= 2
    return v


def kernel(
    nz, nx,
    cache_hbm, qn_hbm, qr_hbm, se_hbm, off_hbm, uk_hbm, uv_hbm, go_hbm,
    dc_ref, dqn_ref, dqr_ref,
    cache_ref, qr_ref, se_ref, off_ref, wide,
    land, full, cT, extT, ext, backT, back, upkT, S, dP, pT, dsT, mx, tot, dl, D,
    csnd, crcv, psnd, prcv, zsnd, zrcv, wsnd, wrcv, fin,
    in_sem, g_send, g_recv, c_send, c_recv, p_send, p_recv, z_send, z_recv,
    w_send, w_recv, f_send, f_recv,
):
    width, own = cache_ref.shape
    hwide, qwide = width // 2, width // 4
    half, quarter = own // 2, own // 4
    pair = 2 * own
    queries = qn_hbm.shape[0]
    heads = qn_hbm.shape[1] // NOPE
    qn_ref, go_ref = wide.at[0:queries], wide.at[queries : 2 * queries]
    uk_ref = wide.at[2 * queries : 2 * queries + LATENT]
    uv_ref = wide.at[2 * queries + LATENT :]
    rows = heads * queries
    scale = (NOPE + ROPE) ** (-0.5)
    s_me = lax.axis_index("seq")
    h_me = lax.axis_index("head")
    z, y = s_me // 2, lax.rem(s_me, 2)
    x, core = h_me // 2, lax.rem(h_me, 2)
    xg, xp = x // 2, lax.rem(x, 2)
    oy, oc, oxp = 1 - y, 1 - core, 1 - xp
    ngroups = nx // 2

    places = (
        (cache_hbm, cache_ref, 0), (se_hbm, se_ref, 1), (off_hbm, off_ref, 2), (qr_hbm, qr_ref, 3),
        (qn_hbm, qn_ref, 4), (uk_hbm, uk_ref, 4), (go_hbm, go_ref, 4), (uv_hbm, uv_ref, 4),
    )
    loads = [pltpu.make_async_copy(src, dst, in_sem.at[i]) for src, dst, i in places]
    loads[0].start()

    def at(zz, yy, xx, cc):
        return (zz * 2 + yy, xx * 2 + cc)

    xo = xg * 2 + oxp
    zs = [flip(z, k) for k in range(nz)]
    z_devs = [at(zz, y, x, core) for zz in zs]
    y_dev = at(z, oy, x, core)
    x_dev = at(z, y, xo, core)
    xy_dev = at(z, oy, xo, core)
    c_dev = at(z, y, x, oc)
    xc_dev = at(z, y, xo, oc)
    xgs = [lax.rem(xg + k, ngroups) for k in range(ngroups)]
    g_devs = [at(z, y, g * 2 + xp, core) for g in xgs]

    barrier = pltpu.get_barrier_semaphore()
    peers = z_devs[1:] + [y_dev, x_dev, xy_dev, c_dev, xc_dev] + g_devs[1:]
    for dev in peers:
        pl.semaphore_signal(barrier, inc=1, device_id=dev, device_id_type=MESH)
    for load in loads[1:]:
        load.start()
    loads[0].wait()
    pl.semaphore_wait(barrier, len(peers))

    def remote(src, dst, send, recv, dev):
        return pltpu.make_async_remote_copy(
            src_ref=src, dst_ref=dst, send_sem=send, recv_sem=recv,
            device_id=dev, device_id_type=MESH,
        )

    def go(copy):
        copy.start()

    def sent(ref, sem):
        remote(ref, ref, sem, sem, c_dev).wait_send()

    def part(cc, xx):
        return pl.ds(pl.multiple_of(cc * hwide + xx * qwide, 16), qwide)

    def whole(cc):
        return pl.ds(pl.multiple_of(cc * hwide, 16), hwide)

    mine, theirs = part(core, xp), part(core, oxp)

    def gather(src, k, r, rs, sem, dev):
        go(remote(src, land.at[k * 2 + r, rs], g_send.at[0], g_recv.at[sem], dev))

    def pass_on(k, r, rs, sem, dev, to=None):
        gather(land.at[k * 2 + r, rs], k, r if to is None else to, rs, sem, dev)

    def arrived(k, r, rs, sem):
        piece = land.at[k * 2 + r, rs]
        remote(piece, piece, g_send.at[0], g_recv.at[sem], c_dev).wait_recv()

    arrivals = [(0, 0), (0, 1)] + [(k, r) for r in range(2) for k in range(1, nz)]
    groups = [arrivals[i : i + 2] for i in range(0, len(arrivals), 2)]
    group_of = {b: g for g, blocks in enumerate(groups) for b in blocks}

    def from_plane(k, r):
        return nz + k * 2 + r

    def from_core(k, r):
        return 3 * nz + group_of[k, r]

    for k in range(1, nz):
        gather(cache_ref.at[mine], k, 0, mine, k, z_devs[k])
    gather(cache_ref.at[whole(core)], 0, 1, whole(core), 0, y_dev)
    land[0] = cache_ref[...]

    def e_own():
        arrived(0, 1, whole(core), 0)
        pass_on(0, 1, whole(core), from_core(0, 1), c_dev)

    def e_z(k):
        arrived(k, 0, mine, k)
        pass_on(k, 0, mine, from_plane(k, 0), x_dev)
        pass_on(k, 0, mine, from_plane(k, 1), y_dev, 1)
        if k in range(1, nz):
            pass_on(k, 0, mine, from_plane(k, 1), xy_dev, 1)

    def e_h(k, r):
        arrived(k, r, whole(core) if r else theirs, from_plane(k, r))
        if r == 0 and k not in range(1, nz):
            pass_on(k, 0, theirs, from_plane(k, 1), y_dev, 1)
        pass_on(k, r, whole(core), from_core(k, r), c_dev)

    loads[1].wait()
    loads[2].wait()
    factor = jnp.exp2(se_ref[...].astype(F32))
    lane = lax.broadcasted_iota(jnp.int32, (1, queries), 1)
    pos = jnp.zeros((1, queries), jnp.int32)
    for b in range(queries // QBLOCK):
        inside = (lane >= b * QBLOCK) & (lane < (b + 1) * QBLOCK)
        pos = jnp.where(inside, off_ref[b] + lane - b * QBLOCK, pos)
    loads[3].wait()
    pltpu.make_async_copy(wide, wide, in_sem.at[4]).wait()

    for h in range(heads):
        cols = slice(h * NOPE, (h + 1) * NOPE)
        qs = slice(h * queries, (h + 1) * queries)
        w = uk_ref[:, cols]
        a = (dot_nt(w, qn_ref[:, cols]) * factor).astype(BF16)
        extT[0:LATENT, qs] = a
        ext[qs, 0:LATENT] = a.T
        upkT[cols, :] = w.T
        g = dot_nt(uv_ref[:, cols], go_ref[:, cols]).astype(BF16)
        backT[:, qs] = g
        back[qs, :] = g.T
    for h in range(0, heads, 2):
        r = (qr_ref[:, h * ROPE : (h + 2) * ROPE].astype(F32).T * factor).astype(BF16)
        for i in range(2):
            p = r[i * ROPE : (i + 1) * ROPE, :]
            qs = slice((h + i) * queries, (h + i + 1) * queries)
            extT[LATENT:width, qs] = p
            ext[qs, LATENT:width] = p.astype(F32).T.astype(BF16)

    tile = 2 * queries
    pos2 = jnp.concatenate([pos, pos], axis=1)
    tiles = rows // tile

    def rows_of(k, r):
        return slice((k * 2 + r) * own, (k * 2 + r + 1) * own)

    def turn(k, r):
        b = land[k * 2 + r]
        cT[:, rows_of(k, r)] = b
        full[rows_of(k, r), :] = b.T

    def scores(g, t):
        c = jnp.concatenate([full[rows_of(*b), :] for b in groups[g]], axis=0)
        ls = slice(t * tile, (t + 1) * tile)
        s = dot(c, extT[:, ls]) * (scale * math.log2(math.e))
        dp = dot(c[:, :LATENT], backT[:, ls])
        m = jnp.full((8, tile), NEG, F32)
        for i, (k, r) in enumerate(groups[g]):
            base = (zs[k] * 2 + (oy if r else y)) * own
            key = base + lax.broadcasted_iota(jnp.int32, (own, tile), 0)
            si = jnp.where(key <= pos2, s[i * own : (i + 1) * own], NEG)
            S[rows_of(k, r), ls] = si
            m = jnp.maximum(m, jnp.max(si.reshape(own // 8, 8, tile), axis=0))
            dP[rows_of(k, r), ls] = dp[i * own : (i + 1) * own]
        mx[g, :, ls] = m

    def soft(g, t):
        ls = slice(t * tile, (t + 1) * tile)
        top = jnp.max(mx[g, :, ls], axis=0, keepdims=True)
        t8 = jnp.zeros((8, tile), F32)
        d8 = jnp.zeros((8, tile), F32)
        for b in groups[g]:
            rs = rows_of(*b)
            p = jnp.exp2(S[rs, ls] - top)
            S[rs, ls] = p
            t8 = t8 + jnp.sum(p.reshape(own // 8, 8, tile), axis=0)
            d8 = d8 + jnp.sum((p * dP[rs, ls]).reshape(own // 8, 8, tile), axis=0)
        tot[g, :, ls] = t8
        dl[g, :, ls] = d8

    def both(g, first, last):
        for t in range(first, last):
            scores(g, t)
            if t > first:
                soft(g, t - 1)
        soft(g, last - 1)

    def ready(g):
        first = groups[g][0]
        if g == 0:
            arrived(0, 1, whole(oc), from_core(0, 1))
        else:
            two = land.at[0:2, whole(oc)]
            remote(two, two, g_send.at[0], g_recv.at[from_core(*first)], c_dev).wait_recv()
        for b in groups[g]:
            turn(*b)

    e_z(1)
    e_own()
    for k in range(2, nz):
        e_z(k)
    pending = arrivals[2:]

    def forward(g):
        while pending and group_of[pending[0]] <= g:
            e_h(*pending.pop(0))

    ready(0)
    both(0, 0, tiles)
    forward(1)
    for g in range(1, len(groups)):
        forward(g + 1)
        ready(g)
        both(g, 0, tiles)

    tops = [jnp.max(mx[k], axis=0, keepdims=True) for k in range(nz)]
    top = functools.reduce(jnp.maximum, tops)
    parts = [jnp.exp2(t - top) for t in tops]
    total = sum(p * jnp.sum(tot[k], axis=0, keepdims=True) for k, p in enumerate(parts))
    delta = sum(p * jnp.sum(dl[k], axis=0, keepdims=True) for k, p in enumerate(parts))
    inv = 1.0 / total
    delta = delta * inv

    def settle(k, r):
        f = parts[group_of[k, r]] * inv
        rs = rows_of(k, r)
        for h in range(heads):
            ls = slice(h * queries, (h + 1) * queries)
            pr = S[rs, ls] * f[:, ls]
            pT[rs, ls] = pr.astype(BF16)
            dsT[rs, ls] = (pr * (dP[rs, ls] - delta[:, ls]) * scale).astype(BF16)

    def step_piece(k, r):
        rs = rows_of(k, r)
        ds, pb = dsT[rs, :], pT[rs, :]
        v = dot(ds, ext[:, 0:LATENT]) + dot(pb, back[...])
        t = dot(ds, ext[:, LATENT:width])
        n = quarter // 2
        for c in range(2):
            for xx in range(2):
                i = c * half + xx * quarter
                for j in range(LATENT // 128):
                    cols = slice(j * 128, (j + 1) * 128)
                    D[k, r, c, xx, j * quarter : (j + 1) * quarter, :] = v[i : i + quarter, cols]
                tail = jnp.concatenate([t[i : i + n], t[i + n : i + quarter]], axis=1)
                D[k, r, c, xx, LATENT // 128 * quarter :, :] = tail

    parts_of = [((k, r),) for k in range(nz - 1, nz - 1, -1) for r in (1, 0)]
    parts_of += [((k, 1), (k, 0)) for k in range(nz - 1, -1, -1)]

    def core_copy(i):
        k, r = parts_of[i][0]
        at_ = (k,) if len(parts_of[i]) > 1 else (k, r)
        return remote(csnd.at[at_], crcv.at[at_], c_send.at[0], c_recv.at[i], c_dev)

    plane = [(1, xp, y_dev), (0, oxp, x_dev), (1, oxp, xy_dev)]

    def plane_copy(k, i):
        return remote(
            psnd.at[k, i], prcv.at[k, i], p_send.at[0], p_recv.at[k], plane[i][2]
        )

    def z_copy(k):
        return remote(zsnd.at[k], zrcv.at[k], z_send.at[0], z_recv.at[0], z_devs[k])

    def chip_sum(k, r, xx):
        return D[k, r, core, xx] + crcv[k, r, xx].astype(F32)

    def step_d(i):
        then = list(parts_of[i + 1]) if i + 1 < len(parts_of) else []
        for b in parts_of[i]:
            step_piece(*b)
            if then:
                settle(*then.pop(0))
        for b in then:
            settle(*b)
        for k, r in parts_of[i]:
            csnd[k, r] = D[k, r, oc].astype(BF16)
        go(core_copy(i))

    def step_e(i):
        core_copy(i).wait_recv()
        for j in (2, 0, 1):
            for k, r in parts_of[i]:
                if plane[j][0] == r:
                    psnd[k, j] = chip_sum(k, r, plane[j][1]).astype(BF16)
                    go(plane_copy(k, j))

    def step_f(k):
        remote(prcv.at[k], prcv.at[k], p_send.at[0], p_recv.at[k], c_dev).wait_recv()
        u = chip_sum(k, 0, xp)
        for i in range(3):
            u = u + prcv[k, i].astype(F32)
        if k:
            zsnd[k] = u.astype(BF16)
            go(z_copy(k))
        return u

    def grad_ext(h):
        cols = slice(h * queries, (h + 2) * queries)
        g = dot(cT[...], dsT[:, cols])
        extT[0:LATENT, cols] = g[0:LATENT].astype(BF16)
        hi = g[LATENT:width]
        ropes = [hi[:, i * queries : (i + 1) * queries] * factor for i in range(2)]
        dqr_ref[:, h * ROPE : (h + 2) * ROPE] = jnp.concatenate(ropes, axis=0).T.astype(BF16)

    def grad_nope(h):
        for i in range(h, h + 2):
            cols = slice(i * NOPE, (i + 1) * NOPE)
            d = dot(upkT[cols, :], extT[0:LATENT, i * queries : (i + 1) * queries]) * factor
            dqn_ref[:, cols] = d.T.astype(BF16)

    todo = [functools.partial(grad_ext, 0)]
    for h in range(2, heads, 2):
        todo += [functools.partial(grad_ext, h), functools.partial(grad_nope, h - 2)]
    todo += [functools.partial(grad_nope, heads - 2)]

    def some(n):
        for _ in range(n):
            if todo:
                todo.pop(0)()

    for b in parts_of[0]:
        settle(*b)
    waiting = list(range(nz - 1, 0, -1))
    done = 0
    for i in range(len(parts_of)):
        step_d(i)
        while done < i and (len(parts_of[done + 1]) > 1 or done + 1 < i):
            step_e(done)
            done += 1
        if nz > 4 and i > nz:
            step_f(waiting.pop(0))
    some(1)
    for i in range(done, len(parts_of) - 1):
        step_e(i)
    for i, k in enumerate(waiting):
        if 1 and i == 2:
            step_e(len(parts_of) - 1)
        some((1, 1, 1)[i] if i < len((1, 1, 1)) else 0)
        step_f(k)
    some(2)
    v = step_f(0)
    if nz > 1:
        others = zrcv.at[1:nz]
        remote(others, others, z_send.at[0], z_recv.at[0], c_dev).wait_recv()
    for k in range(nz - 1, 0, -1):
        v = v + zrcv[k].astype(F32)
    if ngroups > 1:
        wsnd[...] = v.astype(BF16)
        for k in range(1, ngroups):
            go(remote(wsnd, wrcv.at[xg], w_send.at[k], w_recv.at[xg], g_devs[k]))
        wrcv[xg] = v.astype(BF16)
        for k in range(1, ngroups):
            remote(wsnd, wrcv.at[xgs[k]], w_send.at[k], w_recv.at[xgs[k]], g_devs[k]).wait_recv()
        v = wrcv[0].astype(F32)
        for i in range(1, ngroups):
            v = v + wrcv[i].astype(F32)
    fin[core * 2 + xp] = v.astype(BF16)
    here = fin.at[core * 2 + xp]
    last = [x_dev, xc_dev, c_dev]
    for dev in last:
        go(remote(here, here, f_send.at[0], f_recv.at[0], dev))
    some(len(todo))
    sent(land.at[0 : 2 * nz - 1], g_send.at[0])
    sent(csnd, c_send.at[0])
    sent(psnd, p_send.at[0])
    if nz > 1:
        sent(zsnd.at[1:nz], z_send.at[0])
    for k in range(1, ngroups):
        sent(wsnd, w_send.at[k])
    remote(fin.at[0:3], fin.at[0:3], f_send.at[0], f_recv.at[0], c_dev).wait_recv()
    quarters = [fin[i].astype(F32) for i in range(4)]
    for j in range(LATENT // 128):
        rs = slice(j * quarter, (j + 1) * quarter)
        tall = jnp.concatenate([q[rs] for q in quarters], axis=0)
        dc_ref[j * 128 : (j + 1) * 128, :] = tall.T.astype(BF16)
    rs = slice(LATENT // 128 * quarter, quarter * width // 128)
    tails = [q[rs, i * ROPE : (i + 1) * ROPE] for q in quarters for i in range(2)]
    dc_ref[LATENT:width, :] = jnp.concatenate(tails, axis=0).T.astype(BF16)
    sent(fin.at[0:3], f_send.at[0])


def finish(a, b, c, oa, ob, oc, sem):
    copies = [
        pltpu.make_async_copy(src, dst, sem.at[i])
        for i, (src, dst) in enumerate(((b, ob), (a, oa), (c, oc)))
    ]
    for copy in copies:
        copy.start()
    for copy in copies:
        copy.wait()


def solution(mesh):
    seq, head = mesh.shape["seq"], mesh.shape["head"]
    nz, nx = seq // 2, head // 2

    def per_device(cache, qn, qr, se, off, uk, uv, go):
        own, width = cache.shape
        keys = own * seq
        prow = own // 4 * width // 128
        queries = qn.shape[0]
        heads = qn.shape[1] // NOPE
        rows = heads * queries
        vm = pltpu.VMEM
        dma = pltpu.SemaphoreType.DMA
        vspec = pl.BlockSpec(memory_space=pltpu.VMEM)
        hspec = pl.BlockSpec(memory_space=pl.ANY)
        shapes = ((width, own), qn.shape, qr.shape)
        out = pl.pallas_call(
            functools.partial(kernel, nz, nx),
            out_shape=tuple(vm(s, BF16) for s in shapes),
            in_specs=[hspec] * 8,
            out_specs=(vspec, vspec, vspec),
            scratch_shapes=[
                vm((width, own), BF16), vm(qr.shape, BF16),
                vm((1, queries), jnp.int32), pltpu.SMEM(off.shape, jnp.int32),
                vm((2 * (queries + LATENT), qn.shape[1]), BF16),
                vm((seq, width, own), BF16), vm((keys, width), BF16), vm((width, keys), BF16),
                vm((width, rows), BF16), vm((rows, width), BF16),
                vm((LATENT, rows), BF16), vm((rows, LATENT), BF16),
                vm((heads * NOPE, LATENT), BF16),
                vm((keys, rows), F32), vm((keys, rows), F32),
                vm((keys, rows), BF16), vm((keys, rows), BF16),
                vm((nz, 8, rows), F32), vm((nz, 8, rows), F32), vm((nz, 8, rows), F32),
                vm((nz, 2, 2, 2, prow, 128), F32),
                vm((nz, 2, 2, prow, 128), BF16), vm((nz, 2, 2, prow, 128), BF16),
                vm((nz, 3, prow, 128), BF16), vm((nz, 3, prow, 128), BF16),
                vm((nz, prow, 128), BF16), vm((nz, prow, 128), BF16),
                vm((prow, 128), BF16), vm((nx // 2, prow, 128), BF16),
                vm((4, prow, 128), BF16),
                dma((5,)), dma((1,)), dma((4 * nz,)), dma((1,)), dma((2 * nz,)),
                dma((1,)), dma((nz,)), dma((1,)), dma((1,)),
                dma((nx // 2,)), dma((nx // 2,)), dma((1,)), dma((1,)),
            ],
            compiler_params=pltpu.CompilerParams(
                collective_id=0, has_side_effects=True, vmem_limit_bytes=58 * 1024 * 1024
            ),
        )(cache.T, qn, qr, se.reshape(1, -1), off, uk, uv, go)
        dc, dqn, dqr = pl.pallas_call(
            finish,
            out_shape=tuple(jax.ShapeDtypeStruct(s, BF16) for s in shapes),
            in_specs=[vspec] * 3,
            out_specs=(hspec,) * 3,
            scratch_shapes=[dma((3,))],
            compiler_params=pltpu.CompilerParams(vmem_limit_bytes=1024 * 1024),
        )(*out)
        return dc.T, dqn, dqr

    in_specs = (
        P("seq", None), P("seq", "head"), P("seq", "head"), P("seq"), P("seq"),
        P(None, "head"), P(None, "head"), P("seq", "head"),
    )
    out_specs = (P("seq", None), P("seq", "head"), P("seq", "head"))
    return jax.shard_map(
        per_device, mesh=mesh, in_specs=in_specs, out_specs=out_specs, check_vma=False
    )
```

time: 36.5 us -> 35.2 us (0.964)
  Pallas kernels: 35.7 us -> 34.4 us
    pallas_call x1, Pallas kernels: 34.9 us -> 33.6 us  [per_device(): pl.pallas_call(functools.partial(kernel, nz, nx), out_shape=tuple((vm(s,...]
where the time goes in v3:
time: 35.2 us; the launch traced here: 35 us
  Pallas kernels  34.4 us (98%)
  between operations  0.64 us (2%)
    pallas_call x1, Pallas kernels, per_device(): pl.pallas_call(functools.partial(kernel, nz, nx), out_shape=tuple((vm(s,...  33.6 us
    pallas_call x1, Pallas kernels, per_device(): pl.pallas_call(finish, out_shape=tuple((jax.ShapeDtypeStruct(s, BF16) for...  0.82 us

profile of v3, /device:TPU:0, one launch (start us, length us, event | category | flops | bytes accessed | tf_op | source)
XLA Modules:
  0.0 35.0 jit_solution(3841780055916769471)
XLA Ops:
  0.6 33.6 %shard_map.103 = (bf16[576,128]{1,0:T(8,128)(2,1)S(1)}, bf16[128,1024]{1,0:T(8,128)(2,1)S(1)}, bf16[128,512]{1,0:T(8,128)(2,1)S(1)}) custom-call(bf16[576,128]{1,0:T(8,128)(2,1)} %bitcast.3, bf16[128,1024]{1,0:T(8,128)(2,1)} %qn_hbm.1, bf16[128,512]{1,0:T(8,128)(2,1)} %qr_hbm.1, s32[1,128]{1,0:T(1,128)} %bitcast.4, s32[2]{0:T(128)} %off_hbm.1, ...), custom_call_target="tpu_custom_call" | custom-call | tf_op jit(solution)/shard_map/pallas_call | solution.py:460
  34.2 0.8 %shard_map.104 = (bf16[576,128]{1,0:T(8,128)(2,1)}, bf16[128,1024]{1,0:T(8,128)(2,1)}, bf16[128,512]{1,0:T(8,128)(2,1)}) custom-call(bf16[576,128]{1,0:T(8,128)(2,1)S(1)} %get-tuple-element.9.a, bf16[128,1024]{1,0:T(8,128)(2,1)S(1)} %get-tuple-element.10.b, bf16[128,512]{1,0:T(8,128)(2,1)S(1)} %get-tuple-element.11.c), custom_call_target="tpu_custom_call" | custom-call | tf_op jit(solution)/shard_map/pallas_call | solution.py:490

commit v4 on v3

--- a/solution.py
+++ b/solution.py
@@ -129,14 +129,15 @@
     group_of = {b: g for g, blocks in enumerate(groups) for b in blocks}
 
     def from_plane(k, r):
-        return nz + k * 2 + r
+        return nz + (k - 1) * 2 + r
 
     def from_core(k, r):
-        return 3 * nz + group_of[k, r]
-
-    for k in range(1, nz):
+        return 3 * nz - 2 + group_of[k, r]
+
+    gather(cache_ref.at[mine], 1, 0, mine, 1, z_devs[1])
+    gather(cache_ref.at[whole(core)], 0, 1, whole(core), 0, y_dev)
+    for k in range(2, nz):
         gather(cache_ref.at[mine], k, 0, mine, k, z_devs[k])
-    gather(cache_ref.at[whole(core)], 0, 1, whole(core), 0, y_dev)
     land[0] = cache_ref[...]
 
     def e_own():
@@ -479,7 +480,7 @@
                 vm((nz, prow, 128), BF16), vm((nz, prow, 128), BF16),
                 vm((prow, 128), BF16), vm((nx // 2, prow, 128), BF16),
                 vm((4, prow, 128), BF16),
-                dma((5,)), dma((1,)), dma((4 * nz,)), dma((1,)), dma((2 * nz,)),
+                dma((5,)), dma((1,)), dma((4 * nz - 2,)), dma((1,)), dma((nz,)),
                 dma((1,)), dma((nz,)), dma((1,)), dma((1,)),
                 dma((nx // 2,)), dma((nx // 2,)), dma((1,)), dma((1,)),
             ],

time: 35.2 us -> 35.1 us (level)
  no operation moved by 1% of the time
where the time goes in v4:
time: 35.1 us; the launch traced here: 35 us
  Pallas kernels  34.3 us (98%)
  between operations  0.64 us (2%)
    pallas_call x1, Pallas kernels, per_device(): pl.pallas_call(functools.partial(kernel, nz, nx), out_shape=tuple((vm(s,...  33.5 us
    pallas_call x1, Pallas kernels, per_device(): pl.pallas_call(finish, out_shape=tuple((jax.ShapeDtypeStruct(s, BF16) for...  0.82 us

profile of v4, /device:TPU:0, one launch (start us, length us, event | category | flops | bytes accessed | tf_op | source)
XLA Modules:
  0.0 35.0 jit_solution(5423137527112896911)
XLA Ops:
  0.6 33.5 %shard_map.103 = (bf16[576,128]{1,0:T(8,128)(2,1)S(1)}, bf16[128,1024]{1,0:T(8,128)(2,1)S(1)}, bf16[128,512]{1,0:T(8,128)(2,1)S(1)}) custom-call(bf16[576,128]{1,0:T(8,128)(2,1)} %bitcast.3, bf16[128,1024]{1,0:T(8,128)(2,1)} %qn_hbm.1, bf16[128,512]{1,0:T(8,128)(2,1)} %qr_hbm.1, s32[1,128]{1,0:T(1,128)} %bitcast.4, s32[2]{0:T(128)} %off_hbm.1, ...), custom_call_target="tpu_custom_call" | custom-call | tf_op jit(solution)/shard_map/pallas_call | solution.py:461
  34.2 0.8 %shard_map.104 = (bf16[576,128]{1,0:T(8,128)(2,1)}, bf16[128,1024]{1,0:T(8,128)(2,1)}, bf16[128,512]{1,0:T(8,128)(2,1)}) custom-call(bf16[576,128]{1,0:T(8,128)(2,1)S(1)} %get-tuple-element.9.a, bf16[128,1024]{1,0:T(8,128)(2,1)S(1)} %get-tuple-element.10.b, bf16[128,512]{1,0:T(8,128)(2,1)S(1)} %get-tuple-element.11.c), custom_call_target="tpu_custom_call" | custom-call | tf_op jit(solution)/shard_map/pallas_call | solution.py:491
